TPU v7x, 32 devices: a whole 2x2x4 slice. The times are simulated.
32 devices in a mesh: grp: 2 (over y), kv: 8 (over z, core), hd: 2 (over x), sub: 1.
Axes of the slice: x: 2, y: 2, z: 4, core: 2. Of those that a mesh axis runs over, the one named last changes fastest.
Arguments:
- queries: bfloat16 [256, 8192], P(('grp', 'kv'), 'hd'), parts along dimension 0, may hold values from -12 to 12
- prompt_of: int32 [256, 1], P('grp'), parts along dimension 0, may hold values from 0 to 1; in each aligned block of 16 rows (0 to 15, 16 to 31, ...) at most 8 rows name the same one
- prompt_len: int32 [4], P('grp'), parts along dimension 0, may hold values from 3072 to 4096
- suffix_len: int32 [256], P(('grp', 'kv')), parts along dimension 0, may hold values from 0 to 512
- page_table: int32 [256, 8], P(('grp', 'kv'), 'sub'), parts along dimension 0, may hold values from 0 to 127, as said below
- prompt_keys: bfloat16 [16384, 1024], P(('grp', 'kv', 'sub'), 'hd'), parts along dimension 0, may hold values from -14 to 14
- shared_prompt_values: bfloat16 [16384, 1024], P(('grp', 'kv', 'sub'), 'hd'), parts along dimension 0, may hold values from -6 to 6
- suffix_pool_keys: bfloat16 [2048, 64, 1024], P(('grp', 'kv', 'sub'), None, 'hd'), parts along dimension 0, may hold values from -14 to 14
- suffix_pool_values: bfloat16 [2048, 64, 1024], P(('grp', 'kv', 'sub'), None, 'hd'), parts along dimension 0, may hold values from -6 to 6
Outputs:
- attended: float32 [256, 8192], P(('grp', 'kv'), 'hd'), parts along dimension 0
There are 2 independent parts, one for each index of `grp`. A program takes and returns all parts, laid end to end along the dimension named above; each array names one. Nothing has to cross between parts.
Inputs may be any that keep to these rules, and one draw needn't show every extreme that they name: `prompt_of`: in each aligned block of 16 rows (the sequences of one index of kv), every prompt is named by exactly 8 rows. `page_table`: for each index k of kv and s of sub, the entries in rows k * 16 to (k + 1) * 16 - 1 and columns s * 8 to (s + 1) * 8 - 1 are a permutation of 0 to 127.
All inputs are finite; a program needn't handle non-finite values.
Results may differ from a plain program's by a relative error of at most 0.0011.
Values may be sent and summed in bfloat16 or wider, within the bound.
No kernel may reach another device: no remote copies, remote signals or barrier semaphores. Data moves between devices by JAX's collectives and lax.ppermute only.
A program may use at most 128 MiB of HBM per device.

v0:
```python
import math

import jax
import jax.numpy as jnp
from jax import lax
from jax.sharding import PartitionSpec as P

HEAD_SIZE = 128


NEGATIVE = -1e30


def joined(value, axis, combine):
    everything = jax.tree.map(lambda part: lax.all_gather(part, axis), value)
    leading = jax.tree.map(lambda part: part[0], everything)

    def hop(k, so_far):
        return combine(so_far, jax.tree.map(lambda part: part[k], everything))

    return lax.fori_loop(1, lax.axis_size(axis), hop, leading)


def attend_block(sent_rows, key_block, value_block, lower_bound, upper_bound, first_position):
    row_count = sent_rows.shape[0]
    key_count = key_block.shape[0]
    kv_local = key_block.shape[1] // HEAD_SIZE
    query_group_size = sent_rows.shape[1] // (HEAD_SIZE * kv_local)
    position = first_position + jnp.arange(key_count, dtype=jnp.int32)
    key_mask = (position[None, :] >= lower_bound[:, None]) & (
        position[None, :] < upper_bound[:, None]
    )
    key_mask = key_mask[:, None, :]
    score_scale = 1.0 / math.sqrt(HEAD_SIZE)
    blended_parts = []
    lse_parts = []
    for kv_head in range(kv_local):
        low_column = kv_head * query_group_size * HEAD_SIZE
        head_query = sent_rows[:, low_column : low_column + query_group_size * HEAD_SIZE].reshape(
            row_count * query_group_size, HEAD_SIZE
        )
        head_keys = key_block[:, kv_head * HEAD_SIZE : (kv_head + 1) * HEAD_SIZE]
        head_values = value_block[:, kv_head * HEAD_SIZE : (kv_head + 1) * HEAD_SIZE]
        scores = lax.dot_general(
            head_query, head_keys, (((1,), (1,)), ((), ())), preferred_element_type=jnp.float32
        )
        scores = (scores * score_scale).reshape(row_count, query_group_size, key_count)
        scores = jnp.where(key_mask, scores, NEGATIVE)
        row_max = jnp.max(scores, axis=2, keepdims=True)
        weights = jnp.where(key_mask, jnp.exp(scores - row_max), 0.0)
        totals = jnp.maximum(jnp.sum(weights, axis=2), 1.0)
        weighted = jnp.dot(
            weights.astype(jnp.bfloat16).reshape(row_count * query_group_size, key_count),
            head_values,
            preferred_element_type=jnp.float32,
        )
        weighted = weighted.reshape(row_count, query_group_size, HEAD_SIZE) / totals[:, :, None]
        blended_parts.append(weighted.reshape(row_count, query_group_size * HEAD_SIZE))
        lse_parts.append(row_max[:, :, 0] + jnp.log(totals))
    return (jnp.concatenate(blended_parts, axis=1), jnp.concatenate(lse_parts, axis=1))


def combine_halves(earlier, later):
    joint_max = jnp.maximum(earlier[0], later[0])
    left_factor = jnp.exp(earlier[0] - joint_max)
    right_factor = jnp.exp(later[0] - joint_max)
    totals = earlier[1] * left_factor + later[1] * right_factor
    blended = earlier[2] * left_factor[:, :, None] + later[2] * right_factor[:, :, None]
    return (joint_max, totals, blended)


def shards(
    queries,
    prompt_of,
    prompt_len,
    suffix_len,
    page_table,
    prompt_keys,
    shared_prompt_values,
    suffix_pool_keys,
    suffix_pool_values,
):
    kv_count = lax.axis_size("kv")
    sub_count = lax.axis_size("sub")
    kv_index = lax.axis_index("kv")
    sub_index = lax.axis_index("sub")
    seq_local = queries.shape[0]
    row_width = queries.shape[1]
    heads_local = row_width // HEAD_SIZE
    cache_local = prompt_keys.shape[0]
    kv_reach = sub_count * cache_local
    prompt_count = prompt_len.shape[0]
    prompt_starts = jnp.cumsum(prompt_len) - prompt_len
    prompt_ends = prompt_starts + prompt_len
    prompt_labels = jnp.arange(prompt_count, dtype=jnp.int32)
    range_low = jnp.arange(kv_count, dtype=jnp.int32) * kv_reach
    intersections = (prompt_starts[None, :] < range_low[:, None] + kv_reach) & (
        prompt_ends[None, :] > range_low[:, None]
    )
    later_slot = prompt_starts[None, :] > range_low[:, None]
    first_position = (kv_index * sub_count + sub_index) * cache_local
    most_rows = seq_local // prompt_count
    owned_prompt = lax.dynamic_slice_in_dim(prompt_of[:, 0], kv_index * seq_local, seq_local)
    prompt_hits = owned_prompt[:, None] == prompt_labels[None, :]
    hit_counts = prompt_hits.astype(jnp.int32)
    ranks = jnp.sum((jnp.cumsum(hit_counts, axis=0) - hit_counts) * hit_counts, axis=1)
    seq_intersection = jnp.any(intersections[:, None, :] & prompt_hits[None, :, :], axis=2)
    seq_later = jnp.any(later_slot[:, None, :] & prompt_hits[None, :, :], axis=2).astype(jnp.int32)
    slot_labels = jnp.arange(2, dtype=jnp.int32)
    rank_labels = jnp.arange(most_rows, dtype=jnp.int32)
    selector = seq_intersection[:, None, None, :] & (
        seq_later[:, None, None, :] == slot_labels[None, :, None, None]
    )
    selector = selector & (ranks[None, None, None, :] == rank_labels[None, None, :, None])
    selector = selector.reshape(kv_count * 2 * most_rows, seq_local)
    outgoing = jnp.dot(
        selector.astype(jnp.bfloat16), queries, preferred_element_type=jnp.float32
    ).astype(jnp.bfloat16)
    incoming = lax.all_to_all(
        outgoing.reshape(kv_count, 2 * most_rows, row_width),
        "kv",
        split_axis=0,
        concat_axis=0,
        tiled=True,
    )
    mine_intersection = lax.dynamic_index_in_dim(intersections, kv_index, 0, keepdims=False)
    mine_later = lax.dynamic_index_in_dim(later_slot, kv_index, 0, keepdims=False).astype(jnp.int32)
    chosen = mine_intersection[None, :] & (mine_later[None, :] == slot_labels[:, None])
    slot_low = jnp.sum(jnp.where(chosen, prompt_starts[None, :], 0), axis=1)
    slot_high = jnp.sum(jnp.where(chosen, prompt_ends[None, :], 0), axis=1)
    lower_bound = jnp.broadcast_to(
        jnp.repeat(slot_low, most_rows)[None, :], (kv_count, 2 * most_rows)
    ).reshape(-1)
    upper_bound = jnp.broadcast_to(
        jnp.repeat(slot_high, most_rows)[None, :], (kv_count, 2 * most_rows)
    ).reshape(-1)
    sent_rows = incoming.reshape(kv_count * 2 * most_rows, row_width)
    back_rows = 2 * most_rows
    prompt_out, prompt_lse = attend_block(
        sent_rows, prompt_keys, shared_prompt_values, lower_bound, upper_bound, first_position
    )
    returned_out, returned_lse = (
        lax.all_to_all(
            prompt_out.reshape(kv_count, back_rows, row_width),
            "kv",
            split_axis=0,
            concat_axis=0,
            tiled=True,
        ),
        lax.all_to_all(
            prompt_lse.reshape(kv_count, back_rows, heads_local),
            "kv",
            split_axis=0,
            concat_axis=0,
            tiled=True,
        ),
    )
    page_slots = page_table.shape[1]
    page_length = suffix_pool_keys.shape[1]
    suffix_span = page_slots * page_length
    gathered_keys = suffix_pool_keys[page_table].reshape(seq_local, suffix_span, -1)
    gathered_values = suffix_pool_values[page_table].reshape(seq_local, suffix_span, -1)
    suffix_first = sub_index * suffix_span

    def one_sequence(query_line, seq_keys, seq_values, seq_length):
        return attend_block(
            query_line[None, :],
            seq_keys,
            seq_values,
            jnp.zeros((1,), jnp.int32),
            seq_length[None],
            suffix_first,
        )

    suffix_out, suffix_lse = jax.vmap(one_sequence)(
        queries, gathered_keys, gathered_values, suffix_len
    )
    suffix_out = suffix_out[:, 0].reshape(seq_local, heads_local, HEAD_SIZE)
    suffix_lse = suffix_lse[:, 0]
    flat_lse = returned_lse.reshape(-1, heads_local)
    flat_out = returned_out.reshape(-1, heads_local, HEAD_SIZE)
    masked_lse = jnp.where(selector[:, :, None], flat_lse[:, None, :], NEGATIVE)
    joint_max = jnp.maximum(jnp.max(masked_lse, axis=0), suffix_lse)
    factors = jnp.where(selector[:, :, None], jnp.exp(masked_lse - joint_max[None]), 0.0)
    own_factor = jnp.exp(suffix_lse - joint_max)
    totals = jnp.sum(factors, axis=0) + own_factor
    blended = jnp.einsum("rsh,rhd->shd", factors, flat_out, precision=lax.Precision.HIGHEST)
    blended = blended + own_factor[:, :, None] * suffix_out
    joint_max, totals, blended = joined((joint_max, totals, blended), "sub", combine_halves)
    return (blended / totals[:, :, None]).reshape(seq_local, row_width).astype(jnp.float32)


def solution(mesh):
    placed = (
        P(("grp", "kv"), "hd"),
        P("grp", None),
        P("grp"),
        P(("grp", "kv")),
        P(("grp", "kv"), "sub"),
        P(("grp", "kv", "sub"), "hd"),
        P(("grp", "kv", "sub"), "hd"),
        P(("grp", "kv", "sub"), None, "hd"),
        P(("grp", "kv", "sub"), None, "hd"),
    )
    return jax.shard_map(
        shards, mesh=mesh, in_specs=placed, out_specs=P(("grp", "kv"), "hd"), check_vma=False
    )
```

profile of v0, /device:TPU:0, one launch (start us, length us, event | category | flops | bytes accessed | tf_op | source)
XLA Modules:
  0.0 137.8 jit_solution(13117448288514897727)
XLA Ops:
  0.0 0.8 reduce-window.8
  0.8 0.7 bitcast_subtract_fusion
  1.7 0.2 select_reduce_fusion.1
  2.4 2.3 %convolution_convert_fusion = bf16[128,4096]{1,0:T(8,128)(2,1)} fusion(pred[128,16]{1,0:T(8,128)(4,1)S(1)} %bitcast.195, bf16[16,4096]{1,0:T(8,128)(2,1)} %param.9), kind=kOutput, calls=%fused_computation.10 | convolution fusion | flops 17301504 | bytes 1181696 | tf_op jit(solution)/shard_map/dot_general | solution.py:116
  4.7 6.4 %all-to-all-start = ((bf16[8,16,4096]{2,1,0:T(8,128)(2,1)}), bf16[8,16,4096]{2,1,0:T(8,128)(2,1)S(1)}, u32[]{:S(2)}, u32[]{:S(2)}) async-start(bf16[8,16,4096]{2,1,0:T(8,128)(2,1)} %bitcast.7), calls=%async_computation | async-start | bytes 2097152 | tf_op jit(solution)/shard_map/all_to_all | solution.py:119
  11.1 0.2 select_reduce_fusion.3
  11.8 0.7 compare_select_fusion
  12.7 0.8 slice_bitcast_fusion.1
  13.5 10.0 %gather_fusion.1 = bf16[128,64,512]{2,1,0:T(8,128)(2,1)} fusion(bf16[128,64,512]{2,1,0:T(8,128)(2,1)} %param.17, s32[1024]{0:T(1024)S(1)} %pad_clamp_fusion), kind=kCustom, calls=%fused_computation.1 | custom fusion | bytes 16777728 | tf_op jit(solution)/shard_map/gather | solution.py:162
  23.5 10.0 %gather_fusion = bf16[128,64,512]{2,1,0:T(8,128)(2,1)} fusion(bf16[128,64,512]{2,1,0:T(8,128)(2,1)} %param.16, s32[1024]{0:T(1024)S(1)} %pad_clamp_fusion), kind=kCustom, calls=%fused_computation | custom fusion | bytes 16777728 | tf_op jit(solution)/shard_map/gather | solution.py:161
  33.6 0.2 compare_and_fusion
  33.8 3.9 %all-to-all-done = bf16[8,16,4096]{2,1,0:T(8,128)(2,1)S(1)} async-done(((bf16[8,16,4096]{2,1,0:T(8,128)(2,1)}), bf16[8,16,4096]{2,1,0:T(8,128)(2,1)S(1)}, u32[]{:S(2)}, u32[]{:S(2)}) %all-to-all-start) | async-done | bytes 1048608 | tf_op jit(solution)/shard_map/all_to_all | solution.py:119
  37.7 0.1 reshape.705
  37.8 0.1 reshape.707
  38.0 0.1 reshape.706
  38.1 2.6 %fusion.130 = f32[1024,1024]{1,0:T(8,128)} fusion(bf16[1024,128]{1,0:T(8,128)(2,1)S(1)} %reshape.707, bf16[1024,512]{1,0:T(8,128)(2,1)S(1)} %copy-done.6), kind=kOutput, calls=%fused_computation.99 | convolution fusion | flops 268435456 | bytes 4718592 | tf_op jit(solution)/shard_map/dot_general | solution.py:44
  40.7 2.7 %fusion.133 = f32[1024,1024]{1,0:T(8,128)} fusion(bf16[1024,128]{1,0:T(8,128)(2,1)S(1)} %reshape.706, bf16[1024,512]{1,0:T(8,128)(2,1)S(1)} %copy-done.6), kind=kOutput, calls=%fused_computation.102 | convolution fusion | flops 268435456 | bytes 4718592 | tf_op jit(solution)/shard_map/dot_general | solution.py:44
  43.5 1.2 fusion
  44.7 1.0 copy-done.2
  45.7 6.4 %fusion.4 = (f32[1024]{0:T(1024)S(1)}, f32[1024]{0:T(1024)S(1)}, f32[1024]{0:T(1024)S(1)}, f32[1024]{0:T(1024)S(1)}, f32[1024,1024]{1,0:T(8,128)S(1)}) fusion(f32[1024,1024]{1,0:T(8,128)S(1)} %get-tuple-element.51, f32[1024]{0:T(1024)S(1)} %get-tuple-element.50, pred[128,1024]{1,0:T(8,128)(4,1)S(1)} %compare_and_fusion, f32[1024,1024]{1,0:T(8,128)} %fusion.130, ...), kind=kOutput, calls=%fused_computation.15 | convolution fusion | flops 283111424 | bytes 17453056 | tf_op jit(solution)/shard_map/dot_general | solution.py:44
  52.1 5.0 %fusion.6 = (f32[1024]{0:T(1024)S(1)}, f32[1024]{0:T(1024)S(1)}, f32[1024]{0:T(1024)S(1)}) fusion(f32[1024,1024]{1,0:T(8,128)S(1)} %copy-done.2, f32[1024]{0:T(1024)S(1)} %get-tuple-element.8, pred[128,1024]{1,0:T(8,128)(4,1)S(1)} %compare_and_fusion, f32[1024]{0:T(1024)S(1)} %get-tuple-element.7, f32[1024,1024]{1,0:T(8,128)S(1)} %copy-done.3, ...), kind=kLoop, calls=%fused_computation.17 | loop fusion | flops 15725568 | bytes 12738560 | tf_op jit(solution)/shard_map/reduce_sum | solution.py:51
  57.2 3.4 %fusion.106 = f32[128,8,128]{2,1,0:T(8,128)S(1)} fusion(f32[1024,1024]{1,0:T(8,128)} %copy-done.5, f32[1024]{0:T(1024)S(1)} %get-tuple-element.6, pred[128,1024]{1,0:T(8,128)(4,1)S(1)} %compare_and_fusion, f32[128,8]{1,0:T(8,128)S(1)} %max.138, bf16[1024,512]{1,0:T(8,128)(2,1)} %param.15), kind=kOutput, calls=%fused_computation.74 | convolution fusion | flops 273809408 | bytes 5120000 | tf_op jit(solution)/shard_map/dot_general | solution.py:52
  60.8 3.2 %fusion.109 = f32[128,8,128]{2,1,0:T(8,128)S(1)} fusion(f32[1024,1024]{1,0:T(8,128)} %fusion.130, f32[1024]{0:T(1024)S(1)} %get-tuple-element.7, pred[128,1024]{1,0:T(8,128)(4,1)S(1)} %compare_and_fusion, f32[128,8]{1,0:T(8,128)S(1)} %max.136, bf16[1024,512]{1,0:T(8,128)(2,1)} %param.15), kind=kOutput, calls=%fused_computation.75 | convolution fusion | flops 273809408 | bytes 5120000 | tf_op jit(solution)/shard_map/dot_general | solution.py:52
  64.2 3.2 %fusion.112 = f32[128,8,128]{2,1,0:T(8,128)S(1)} fusion(f32[1024,1024]{1,0:T(8,128)} %fusion.133, f32[1024]{0:T(1024)S(1)} %get-tuple-element.8, pred[128,1024]{1,0:T(8,128)(4,1)S(1)} %compare_and_fusion, f32[128,8]{1,0:T(8,128)S(1)} %max.134, bf16[1024,512]{1,0:T(8,128)(2,1)} %param.15), kind=kOutput, calls=%fused_computation.76 | convolution fusion | flops 273809408 | bytes 5120000 | tf_op jit(solution)/shard_map/dot_general | solution.py:52
  67.6 3.2 %fusion.115 = f32[128,8,128]{2,1,0:T(8,128)S(1)} fusion(f32[1024,1024]{1,0:T(8,128)} %copy-done.4, f32[1024]{0:T(1024)S(1)} %get-tuple-element.50, pred[128,1024]{1,0:T(8,128)(4,1)S(1)} %compare_and_fusion, f32[128,8]{1,0:T(8,128)S(1)} %max.132, bf16[1024,512]{1,0:T(8,128)(2,1)} %param.15), kind=kOutput, calls=%fused_computation.77 | convolution fusion | flops 273809408 | bytes 5120000 | tf_op jit(solution)/shard_map/dot_general | solution.py:52
  71.2 0.1 pad_maximum_fusion.1
  71.4 0.7 reshape.747
  72.1 3.3 %all-to-all-start.2 = ((f32[8,1,512]{2,1,0:T(1,128)}), f32[8,1,512]{2,1,0:T(1,128)S(1)}, u32[]{:S(2)}, u32[]{:S(2)}) async-start(f32[8,1,512]{2,1,0:T(1,128)} %reshape.747), calls=%async_computation.2 | async-start | bytes 32768 | tf_op jit(solution)/shard_map/all_to_all | solution.py:150
  75.4 1.5 %pad_maximum_fusion = f32[8,16,4096]{2,1,0:T(8,128)} fusion(f32[8,16,1024]{2,1,0:T(8,128)S(1)} %concatenate.25, f32[8,16,1024]{2,1,0:T(8,128)S(1)} %concatenate.24, f32[8,16,1024]{2,1,0:T(8,128)S(1)} %concatenate.23, f32[8,16,1024]{2,1,0:T(8,128)S(1)} %concatenate.22), kind=kLoop, calls=%fused_computation.43 | loop fusion | flops 1572864 | bytes 4194304 | tf_op jit(solution)/shard_map/concatenate | solution.py:60
  76.9 4.1 %all-to-all-done.2 = f32[8,1,512]{2,1,0:T(1,128)S(1)} async-done(((f32[8,1,512]{2,1,0:T(1,128)}), f32[8,1,512]{2,1,0:T(1,128)S(1)}, u32[]{:S(2)}, u32[]{:S(2)}) %all-to-all-start.2) | async-done | bytes 16416 | tf_op jit(solution)/shard_map/all_to_all | solution.py:150
  81.0 3.6 %all-to-all-start.1 = ((f32[8,16,4096]{2,1,0:T(8,128)}), f32[8,16,4096]{2,1,0:T(8,128)S(1)}, u32[]{:S(2)}, u32[]{:S(2)}) async-start(f32[8,16,4096]{2,1,0:T(8,128)} %pad_maximum_fusion), calls=%async_computation.1 | async-start | bytes 4194304 | tf_op jit(solution)/shard_map/all_to_all | solution.py:143
  84.6 2.3 %fusion.191 = (f32[16,8]{1,0:T(8,128)S(1)}, f32[16,8,512]{2,1,0:T(8,128)S(1)}) fusion(bf16[16,8,128]{2,1,0:T(8,128)(2,1)S(1)} %bitcast.206, bf16[16,512,512]{2,1,0:T(8,128)(2,1)} %bitcast.187, pred[16,512]{1,0:T(8,128)(4,1)S(1)} %iota_compare_fusion), kind=kOutput, calls=%fused_computation.201 | convolution fusion | flops 16973696 | bytes 2400768 | tf_op jit(solution)/shard_map/vmap()/dot_general | solution.py:44
  86.9 2.3 %fusion.192 = (f32[16,8]{1,0:T(8,128)S(1)}, f32[16,8,512]{2,1,0:T(8,128)S(1)}) fusion(bf16[16,8,128]{2,1,0:T(8,128)(2,1)S(1)} %bitcast.208, bf16[16,512,512]{2,1,0:T(8,128)(2,1)} %bitcast.188, pred[16,512]{1,0:T(8,128)(4,1)S(1)} %iota_compare_fusion), kind=kOutput, calls=%fused_computation.202 | convolution fusion | flops 16973696 | bytes 2400768 | tf_op jit(solution)/shard_map/vmap()/dot_general | solution.py:44
  89.3 2.3 %fusion.193 = (f32[16,8]{1,0:T(8,128)S(1)}, f32[16,8,512]{2,1,0:T(8,128)S(1)}) fusion(bf16[16,8,128]{2,1,0:T(8,128)(2,1)S(1)} %bitcast.207, bf16[16,512,512]{2,1,0:T(8,128)(2,1)} %bitcast.189, pred[16,512]{1,0:T(8,128)(4,1)S(1)} %iota_compare_fusion), kind=kOutput, calls=%fused_computation.203 | convolution fusion | flops 16973696 | bytes 2400768 | tf_op jit(solution)/shard_map/vmap()/dot_general | solution.py:44
  91.6 2.3 %fusion.194 = (f32[16,8]{1,0:T(8,128)S(1)}, f32[16,8,512]{2,1,0:T(8,128)S(1)}) fusion(bf16[16,8,128]{2,1,0:T(8,128)(2,1)S(1)} %bitcast.205, bf16[16,512,512]{2,1,0:T(8,128)(2,1)} %bitcast.190, pred[16,512]{1,0:T(8,128)(4,1)S(1)} %iota_compare_fusion), kind=kOutput, calls=%fused_computation.204 | convolution fusion | flops 16973696 | bytes 2400768 | tf_op jit(solution)/shard_map/vmap()/dot_general | solution.py:44
  93.9 0.4 fusion.139
  94.3 2.0 %fusion.103 = f32[16,8,128]{2,1,0:T(8,128)S(1)} fusion(bf16[16,512,512]{2,1,0:T(8,128)(2,1)} %bitcast.183, f32[16,8,512]{2,1,0:T(8,128)S(1)} %get-tuple-element.54, f32[16,8]{1,0:T(8,128)S(1)} %get-tuple-element.53, pred[16,512]{1,0:T(8,128)(4,1)S(1)} %iota_compare_fusion, f32[16,8]{1,0:T(8,128)S(1)} %get-tuple-element.37), kind=kOutput, calls=%fused_computation.73 | convolution fusion | flops 16990208 | bytes 2434048 | tf_op jit(solution)/shard_map/vmap()/dot_general | solution.py:52
  96.4 2.0 %fusion.100 = f32[16,8,128]{2,1,0:T(8,128)S(1)} fusion(bf16[16,512,512]{2,1,0:T(8,128)(2,1)} %bitcast.184, f32[16,8,512]{2,1,0:T(8,128)S(1)} %get-tuple-element.60, f32[16,8]{1,0:T(8,128)S(1)} %get-tuple-element.59, pred[16,512]{1,0:T(8,128)(4,1)S(1)} %iota_compare_fusion, f32[16,8]{1,0:T(8,128)S(1)} %get-tuple-element.63), kind=kOutput, calls=%fused_computation.72 | convolution fusion | flops 16990208 | bytes 2434048 | tf_op jit(solution)/shard_map/vmap()/dot_general | solution.py:52
  98.5 2.0 %fusion.97 = f32[16,8,128]{2,1,0:T(8,128)S(1)} fusion(bf16[16,512,512]{2,1,0:T(8,128)(2,1)} %bitcast.185, f32[16,8,512]{2,1,0:T(8,128)S(1)} %get-tuple-element.58, f32[16,8]{1,0:T(8,128)S(1)} %get-tuple-element.57, pred[16,512]{1,0:T(8,128)(4,1)S(1)} %iota_compare_fusion, f32[16,8]{1,0:T(8,128)S(1)} %get-tuple-element.33), kind=kOutput, calls=%fused_computation.71 | convolution fusion | flops 16990208 | bytes 2434048 | tf_op jit(solution)/shard_map/vmap()/dot_general | solution.py:52
  100.5 2.0 %fusion.94 = f32[16,8,128]{2,1,0:T(8,128)S(1)} fusion(bf16[16,512,512]{2,1,0:T(8,128)(2,1)} %bitcast.186, f32[16,8,512]{2,1,0:T(8,128)S(1)} %get-tuple-element.56, f32[16,8]{1,0:T(8,128)S(1)} %get-tuple-element.55, pred[16,512]{1,0:T(8,128)(4,1)S(1)} %iota_compare_fusion, f32[16,8]{1,0:T(8,128)S(1)} %get-tuple-element.65), kind=kOutput, calls=%fused_computation.70 | convolution fusion | flops 16990208 | bytes 2434048 | tf_op jit(solution)/shard_map/vmap()/dot_general | solution.py:52
  103.0 0.5 broadcast.458
  103.5 0.7 reduce.24
  104.3 0.2 select_reduce_fusion
  104.5 0.2 fusion.120
  104.8 28.8 %all-to-all-done.1 = f32[8,16,4096]{2,1,0:T(8,128)S(1)} async-done(((f32[8,16,4096]{2,1,0:T(8,128)}), f32[8,16,4096]{2,1,0:T(8,128)S(1)}, u32[]{:S(2)}, u32[]{:S(2)}) %all-to-all-start.1) | async-done | bytes 2097184 | tf_op jit(solution)/shard_map/all_to_all | solution.py:143
  133.6 0.4 copy.73
  133.9 3.1 %fusion.55 = f32[32,2,8,128]{3,2,1,0:T(8,128)S(1)} fusion(f32[128,32,128]{2,1,0:T(8,128)S(1)} %bitcast.182, f32[16,32,128]{2,1,0:T(8,128)S(1)} %bitcast.192, f32[16,32]{0,1:T(8,128)S(1)} %get-tuple-element.20, f32[16,32]{0,1:T(8,128)S(1)} %get-tuple-element.21, f32[16,32]{0,1:T(8,128)S(1)} %fusion.167, f32[128,32]{0,1:T(8,128)S(1)} %copy.63, ...), kind=kOutput, calls=%fused_computation.57 | convolution fusion | flops 101056512 | bytes 2646016 | tf_op jit(solution)/shard_map/rsh,rhd->shd/dot_general | solution.py:187
  137.1 0.7 copy.93
  (82 shorter events, 3.4 us)
Async XLA Ops:
  0.0 1.5 %copy-start = (s32[128,1]{0,1:T(1,128)S(1)}, s32[128,1]{0,1:T(1,128)}, u32[]{:S(2)}) copy-start(s32[128,1]{0,1:T(1,128)} %param.10) | copy-start | bytes 1540
  4.7 32.9 %all-to-all-start = ((bf16[8,16,4096]{2,1,0:T(8,128)(2,1)}), bf16[8,16,4096]{2,1,0:T(8,128)(2,1)S(1)}, u32[]{:S(2)}, u32[]{:S(2)}) async-start(bf16[8,16,4096]{2,1,0:T(8,128)(2,1)} %bitcast.7), calls=%async_computation | async-start | bytes 2097152 | tf_op jit(solution)/shard_map/all_to_all | solution.py:119
  23.5 10.0 %copy-start.7 = (s32[16]{0:T(128)S(1)}, s32[16]{0:T(128)}, u32[]{:S(2)}) copy-start(s32[16]{0:T(128)} %param.12) | copy-start | bytes 196
  33.4 4.6 %copy-start.6 = (bf16[1024,512]{1,0:T(8,128)(2,1)S(1)}, bf16[1024,512]{1,0:T(8,128)(2,1)}, u32[]{:S(2)}) copy-start(bf16[1024,512]{1,0:T(8,128)(2,1)} %param.14) | copy-start | bytes 3145732
  43.5 2.2 %copy-start.2 = (f32[1024,1024]{1,0:T(8,128)S(1)}, f32[1024,1024]{1,0:T(8,128)}, u32[]{:S(2)}) copy-start(f32[1024,1024]{1,0:T(8,128)} %fusion.133) | copy-start | bytes 12582916
  44.7 7.4 %copy-start.4 = (f32[1024,1024]{1,0:T(8,128)}, f32[1024,1024]{1,0:T(8,128)S(1)}, u32[]{:S(2)}) copy-start(f32[1024,1024]{1,0:T(8,128)S(1)} %get-tuple-element.51) | copy-start | bytes 12582916
  45.7 6.4 %copy-start.3 = (f32[1024,1024]{1,0:T(8,128)S(1)}, f32[1024,1024]{1,0:T(8,128)}, u32[]{:S(2)}) copy-start(f32[1024,1024]{1,0:T(8,128)} %fusion.130) | copy-start | bytes 12582916
  52.1 5.0 %copy-start.5 = (f32[1024,1024]{1,0:T(8,128)}, f32[1024,1024]{1,0:T(8,128)S(1)}, u32[]{:S(2)}) copy-start(f32[1024,1024]{1,0:T(8,128)S(1)} %get-tuple-element.52) | copy-start | bytes 12582916
  72.1 8.9 %all-to-all-start.2 = ((f32[8,1,512]{2,1,0:T(1,128)}), f32[8,1,512]{2,1,0:T(1,128)S(1)}, u32[]{:S(2)}, u32[]{:S(2)}) async-start(f32[8,1,512]{2,1,0:T(1,128)} %reshape.747), calls=%async_computation.2 | async-start | bytes 32768 | tf_op jit(solution)/shard_map/all_to_all | solution.py:150
  81.0 52.6 %all-to-all-start.1 = ((f32[8,16,4096]{2,1,0:T(8,128)}), f32[8,16,4096]{2,1,0:T(8,128)S(1)}, u32[]{:S(2)}, u32[]{:S(2)}) async-start(f32[8,16,4096]{2,1,0:T(8,128)} %pad_maximum_fusion), calls=%async_computation.1 | async-start | bytes 4194304 | tf_op jit(solution)/shard_map/all_to_all | solution.py:143
  102.6 35.2 %copy-start.1 = (s32[128,1]{0,1:T(1,128)S(1)}, s32[128,1]{0,1:T(1,128)}, u32[]{:S(2)}) copy-start(s32[128,1]{0,1:T(1,128)} %param.10) | copy-start | bytes 1540
where the time goes:
time: 139 us; the launch traced here: 138 us
  matrix products  48.7 us (35%)
  waiting for transfers between devices  36.7 us (26%)
  local copies, waits for them, and re-layouts  27.3 us (20%)
  starting transfers between devices  13.3 us (10%)
  other arithmetic  11.3 us (8%)
    all_to_all x1, waiting for transfers between devices, shards(): lax.all_to_all(prompt_out.reshape(kv_count, back_rows, row_width), 'kv',...  28.8 us
    dot_general x8, matrix products, attend_block(): lax.dot_general(head_query, head_keys, (((1,), (1,)), ((), ())), preferre...  22.2 us
    dot_general x8, matrix products, attend_block(): jnp.dot(weights.astype(jnp.bfloat16).reshape(row_count * query_group_size...  21.1 us
    gather x1, local copies, waits for them, and re-layouts, shards(): suffix_pool_values[page_table].reshape(seq_local, suffix_span, -1)  9.96 us
    gather x1, local copies, waits for them, and re-layouts, shards(): suffix_pool_keys[page_table].reshape(seq_local, suffix_span, -1)  9.96 us
    all_to_all x1, starting transfers between devices, shards(): lax.all_to_all(outgoing.reshape(kv_count, 2 * most_rows, row_width), 'kv'...  6.37 us
    reduce_sum x2, other arithmetic, attend_block(): totals = jnp.maximum(jnp.sum(weights, axis=2), 1.0)  5.36 us
    all_to_all x1, waiting for transfers between devices, shards(): lax.all_to_all(prompt_lse.reshape(kv_count, back_rows, heads_local), 'kv'...  4.09 us
  transfers between devices with their start and end apart: 3, of which 3 were waited for; matrix products, arithmetic and copies ran while one was open for 32% of the time, Pallas kernels for 0%

commit v1 on v0

--- a/solution.py
+++ b/solution.py
@@ -1,8 +1,11 @@
+import functools
 import math
 
 import jax
 import jax.numpy as jnp
 from jax import lax
+from jax.experimental import pallas as pl
+from jax.experimental.pallas import tpu as pltpu
 from jax.sharding import PartitionSpec as P
 
 HEAD_SIZE = 128
@@ -190,6 +193,456 @@
     return (blended / totals[:, :, None]).reshape(seq_local, row_width).astype(jnp.float32)
 
 
+LANES = 128
+WIRE = jnp.int16
+WIRE_TOP = 32000.0
+FRACTION_TOP = 32767.0
+LOG2E = math.log2(math.e)
+
+
+def dot_nt(a, b):
+    return lax.dot_general(a, b, (((1,), (1,)), ((), ())), preferred_element_type=jnp.float32)
+
+
+def packed_places(prompt_ref, seqs, group, visit):
+    base = lax.axis_index("kv") * seqs
+    half = seqs // 2
+    front = jnp.int32(0)
+    back = jnp.int32(half)
+    for i in range(seqs):
+        mine = prompt_ref[base + i] == group
+        visit(i, jnp.where(mine, front, back))
+        front = front + jnp.where(mine, 1, 0)
+        back = back + jnp.where(mine, 0, 1)
+
+
+def own_group():
+    return lax.axis_index("kv") // (lax.axis_size("kv") // 2)
+
+
+def pack_kernel(prompt_ref, q_ref, keep_ref, send_ref):
+    seqs, width = q_ref.shape
+    half = width // 2
+    core = lax.axis_index("kv") % 2
+    lane = lax.broadcasted_iota(jnp.int32, (seqs, LANES), 1)
+    row = lax.broadcasted_iota(jnp.int32, (seqs, LANES), 0)
+    place = jnp.full((seqs, LANES), -1, jnp.int32)
+    dests = []
+    packed_places(prompt_ref, seqs, own_group(), lambda i, d: dests.append(d))
+    for i, d in enumerate(dests):
+        place = jnp.where(lane == i, d, place)
+    selector = jnp.where(place == row, 1.0, 0.0).astype(jnp.bfloat16)[:, :seqs]
+    for ref, which in ((keep_ref, core), (send_ref, 1 - core)):
+        block = q_ref[:, pl.ds(pl.multiple_of(which * half, LANES), half)]
+        ref[...] = jnp.dot(selector, block, preferred_element_type=jnp.float32).astype(jnp.bfloat16)
+
+
+def build_kernel(keep_ref, recv_ref, main_ref, cross_ref):
+    rows = keep_ref.shape[0] // 2
+    keep = keep_ref[...].astype(jnp.float32)
+    recv = recv_ref[...].astype(jnp.float32)
+    main_ref[...] = jnp.concatenate([keep[:rows], recv[:rows]], axis=0).astype(jnp.bfloat16)
+    cross_ref[...] = jnp.concatenate([keep[rows:], recv[rows:]], axis=0).astype(jnp.bfloat16)
+
+
+def suffix_kernel(
+    first, prompt_ref, table_ref, length_ref, q_ref, k_hbm, v_hbm, o_ref, l_ref, order, kbuf, vbuf, ksem, vsem
+):
+    seqs, heads, head_size = q_ref.shape
+    count, slots, page, width = kbuf.shape
+    kv_heads = width // head_size
+    group = heads // kv_heads
+    span = slots * page
+
+    def note(i, d):
+        order[d] = jnp.int32(i)
+
+    packed_places(prompt_ref, seqs, own_group(), note)
+    for r in range(count):
+        i = order[first + r]
+        for j in range(slots):
+            entry = table_ref[i, j]
+            pltpu.make_async_copy(k_hbm.at[entry], kbuf.at[r, j], ksem.at[r]).start()
+            pltpu.make_async_copy(v_hbm.at[entry], vbuf.at[r, j], vsem.at[r]).start()
+    position = lax.broadcasted_iota(jnp.int32, (heads, span), 1)
+    scale = 1.0 / math.sqrt(head_size)
+    for r in range(count):
+        i = order[first + r]
+        pltpu.make_async_copy(kbuf.at[r], kbuf.at[r], ksem.at[r]).wait()
+        pltpu.make_async_copy(vbuf.at[r], vbuf.at[r], vsem.at[r]).wait()
+        q = q_ref[i]
+        keys = kbuf[r].reshape(span, width)
+        values = vbuf[r].reshape(span, width)
+        scores = jnp.concatenate(
+            [
+                dot_nt(
+                    q[h * group : (h + 1) * group], keys[:, h * head_size : (h + 1) * head_size]
+                )
+                for h in range(kv_heads)
+            ],
+            axis=0,
+        )
+        keep = position < length_ref[i]
+        scores = jnp.where(keep, scores * scale, NEGATIVE)
+        top = jnp.max(scores, axis=1, keepdims=True)
+        weights = jnp.where(keep, jnp.exp(scores - top), 0.0)
+        total = jnp.maximum(jnp.sum(weights, axis=1, keepdims=True), 1.0)
+        rounded = weights.astype(jnp.bfloat16)
+        out = jnp.concatenate(
+            [
+                jnp.dot(
+                    rounded[h * group : (h + 1) * group],
+                    values[:, h * head_size : (h + 1) * head_size],
+                    preferred_element_type=jnp.float32,
+                )
+                for h in range(kv_heads)
+            ],
+            axis=0,
+        )
+        out = out / total
+        lse = jnp.broadcast_to(top + jnp.log(total), (heads, head_size))
+        for a in range(heads):
+            columns = slice(a * head_size, (a + 1) * head_size)
+            o_ref[r : r + 1, columns] = out[a : a + 1]
+            l_ref[r : r + 1, columns] = lse[a : a + 1]
+
+
+def prompt_kernel(
+    core_ref, length_ref, *refs
+):
+    queries, extras = refs[0:4], refs[4:8]
+    k_own, k_other, v_own, v_other = refs[8:12]
+    own_out, outs, extra_outs = refs[12], refs[13:16], refs[16:20]
+    kcat, vcat, qs, own_side, side, extra_side = refs[20:26]
+    step = pl.program_id(0)
+    rows, columns = queries[0].shape
+    reach, head_size = k_own.shape
+    group = columns // head_size
+    heads = group * pl.num_programs(0)
+    index = lax.axis_index("kv")
+    core = index % 2
+    chip = index // 2
+    ours = own_group()
+    first = chip * 2 * reach
+    starts = (jnp.int32(0), length_ref[0])
+    ends = (length_ref[0], length_ref[0] + length_ref[1])
+    low = jnp.where(ours == 0, starts[0], starts[1])
+    high = jnp.where(ours == 0, ends[0], ends[1])
+    kcat[pl.ds(pl.multiple_of(core * reach, LANES), reach), :] = k_own[...]
+    kcat[pl.ds(pl.multiple_of((1 - core) * reach, LANES), reach), :] = k_other[...]
+    vcat[pl.ds(pl.multiple_of(core * reach, LANES), reach), :] = v_own[...]
+    vcat[pl.ds(pl.multiple_of((1 - core) * reach, LANES), reach), :] = v_other[...]
+    scale = 1.0 / math.sqrt(head_size)
+    lane = lax.broadcasted_iota(jnp.int32, (rows, LANES), 1)
+
+    def attend(sources, blocks, lower, upper, deliver):
+        for g in range(group):
+            for t, source in enumerate(sources):
+                qs[(g * 4 + t) * rows : (g * 4 + t + 1) * rows, :] = source[
+                    :, g * head_size : (g + 1) * head_size
+                ]
+        per = 2
+        chunk = per * 4 * rows
+        for c in range(group // per):
+            block_queries = qs[c * chunk : (c + 1) * chunk, :]
+            parts = []
+            for b in blocks:
+                position = first + b * reach + lax.broadcasted_iota(jnp.int32, (1, reach), 1)
+                bias = jnp.where((position >= lower) & (position < upper), 0.0, NEGATIVE)
+                scores = dot_nt(block_queries, kcat[b * reach : (b + 1) * reach, :]) + bias
+                top = jnp.max(scores, axis=1, keepdims=True)
+                weights = jnp.exp2((scores - top) * (scale * LOG2E))
+                total = jnp.sum(weights, axis=1, keepdims=True)
+                out = jnp.dot(
+                    weights.astype(jnp.bfloat16),
+                    vcat[b * reach : (b + 1) * reach, :],
+                    preferred_element_type=jnp.float32,
+                )
+                parts.append((out / total, top * scale + jnp.log(total)))
+            out, lse = parts[0]
+            if len(parts) > 1:
+                joint = jnp.maximum(parts[0][1], parts[1][1])
+                left = jnp.exp(parts[0][1] - joint)
+                right = jnp.exp(parts[1][1] - joint)
+                total = left + right
+                out = parts[0][0] * (left / total) + parts[1][0] * (right / total)
+                lse = joint + jnp.log(total)
+            for gg in range(per):
+                g = c * per + gg
+                for t in range(4):
+                    at = (gg * 4 + t) * rows
+                    deliver(t, g, out[at : at + rows], lse[at : at + rows])
+
+    def place(ref, g):
+        return ref, pl.ds(pl.multiple_of(step * columns + g * head_size, LANES), head_size)
+
+    def encode(ref, side_ref, t, g, out, lse):
+        head = step * group + g
+        peak = jnp.max(jnp.abs(out), axis=1, keepdims=True)
+        power = jnp.ceil(jnp.clip(jnp.log(jnp.maximum(peak, 1e-30)) * LOG2E, -90.0, 20.0))
+        coded = jnp.round(out * (jnp.exp2(-power) * WIRE_TOP))
+        target, where = place(ref, g)
+        target[:, where] = coded.astype(jnp.int32).astype(WIRE)
+        eighths = jnp.maximum(lse, -4000.0) * 8.0
+        whole = jnp.floor(eighths)
+        fraction = jnp.round((eighths - whole) * FRACTION_TOP)
+        at = slice(t * rows, (t + 1) * rows)
+        held = side_ref[at, :]
+        held = jnp.where(lane == head, whole, held)
+        held = jnp.where(lane == heads + head, fraction, held)
+        side_ref[at, :] = jnp.where(lane == 2 * heads + head, power, held)
+
+    def deliver_main(t, g, out, lse):
+        if t == 0:
+            target, where = place(own_out, g)
+            target[:, where] = out
+            own_side[...] = jnp.where(lane == step * group + g, lse, own_side[...])
+        else:
+            encode(outs[t - 1], side, t - 1, g, out, lse)
+
+    def deliver_extra(t, g, out, lse):
+        encode(extra_outs[t], extra_side, t, g, out, lse)
+
+    @pl.when(step == 0)
+    def _():
+        own_side[...] = jnp.zeros_like(own_side)
+        side[...] = jnp.zeros_like(side)
+        extra_side[...] = jnp.zeros_like(extra_side)
+
+    attend(queries, (0, 1), low, high, deliver_main)
+    straddles = chip == lax.axis_size("kv") // 4 - 1
+
+    @pl.when(straddles)
+    def _():
+        attend(extras, (1,), starts[1], ends[1], deliver_extra)
+
+    @pl.when(step == pl.num_programs(0) - 1)
+    def _():
+        width = heads * head_size
+        own_out[:, width:] = own_side[...]
+        for t, ref in enumerate(outs):
+            ref[:, width:] = side[t * rows : (t + 1) * rows, :].astype(jnp.int32).astype(WIRE)
+        for t, ref in enumerate(extra_outs):
+            ref[:, width:] = extra_side[t * rows : (t + 1) * rows, :].astype(jnp.int32).astype(WIRE)
+
+
+def merge_kernel(own_ref, near_ref, far_ref, both_ref, x_local, x_a, x_b, x_c, keep_ref, send_ref, x_ref):
+    rows, padded = own_ref.shape
+    width = padded - LANES
+    head_size = HEAD_SIZE
+    heads = width // head_size
+    half = rows // 2
+    chip = lax.axis_index("kv") // 2
+    chips = lax.axis_size("kv") // 2
+    for at, ref in enumerate((x_a, x_local, x_b, x_c)):
+
+        @pl.when(chip == at)
+        def _():
+            x_ref[...] = ref[...]
+
+    def decoded(ref):
+        side = ref[:, width:].astype(jnp.int32).astype(jnp.float32)
+        lse = (side[:, :heads] + side[:, heads : 2 * heads] * (1.0 / FRACTION_TOP)) * 0.125
+        return lse, jnp.exp2(side[:, 2 * heads : 3 * heads]) * (1.0 / WIRE_TOP), ref
+
+    own = (own_ref[:, width : width + heads], None, own_ref)
+    x = decoded(x_ref)
+    upper = chip >= chips // 2
+    absent = jnp.full_like(x[0], NEGATIVE)
+    for at, parts in (
+        (0, (own, decoded(near_ref), (jnp.where(upper, x[0], absent), x[1], x[2]))),
+        (half, (decoded(far_ref), decoded(both_ref), (jnp.where(upper, absent, x[0]), x[1], x[2]))),
+    ):
+        joint = functools.reduce(jnp.maximum, [part[0] for part in parts])
+        factors = [jnp.exp(part[0] - joint) for part in parts]
+        total = functools.reduce(jnp.add, factors)
+        shares = [
+            factor / total if part[1] is None else factor / total * part[1]
+            for factor, part in zip(factors, parts)
+        ]
+        lse = joint + jnp.log(total)
+        lse = jnp.concatenate([lse, jnp.zeros((rows, LANES - heads), jnp.float32)], axis=1)
+        keep_ref[at : at + half, width:] = lse[:half]
+        send_ref[at : at + half, width:] = lse[half:]
+        for h in range(heads):
+            columns = slice(h * head_size, (h + 1) * head_size)
+            out = jnp.zeros((rows, head_size), jnp.float32)
+            for share, part in zip(shares, parts):
+                held = part[2][:, columns]
+                if part[1] is not None:
+                    held = held.astype(jnp.int32).astype(jnp.float32)
+                out = out + share[:, h : h + 1] * held
+            keep_ref[at : at + half, columns] = out[:half]
+            send_ref[at : at + half, columns] = out[half:]
+
+
+def final_kernel(prompt_ref, keep_ref, recv_ref, so_a, sl_a, so_b, sl_b, out_ref, acc):
+    seqs, width = out_ref.shape
+    half_width = keep_ref.shape[1] - LANES
+    heads = half_width // HEAD_SIZE
+    half = seqs // 2
+    core = lax.axis_index("kv") % 2
+    for ref, which in ((keep_ref, core), (recv_ref, 1 - core)):
+        for h in range(heads):
+            where = pl.ds(pl.multiple_of(which * half_width + h * HEAD_SIZE, LANES), HEAD_SIZE)
+            for at, so, sl in ((0, so_a, sl_a), (half, so_b, sl_b)):
+                lse = ref[at : at + half, half_width + h : half_width + h + 1]
+                suffix_lse = sl[:, where]
+                joint = jnp.maximum(lse, suffix_lse)
+                left = jnp.exp(lse - joint)
+                right = jnp.exp(suffix_lse - joint)
+                held = ref[at : at + half, h * HEAD_SIZE : (h + 1) * HEAD_SIZE]
+                acc[at : at + half, where] = (left * held + right * so[:, where]) / (left + right)
+
+    dests = []
+    packed_places(prompt_ref, seqs, own_group(), lambda i, d: dests.append(d))
+    for i, d in enumerate(dests):
+        out_ref[i : i + 1, :] = acc[pl.ds(d, 1), :]
+
+
+def split_heads_shards(
+    queries,
+    prompt_of,
+    prompt_len,
+    suffix_len,
+    page_table,
+    prompt_keys,
+    shared_prompt_values,
+    suffix_pool_keys,
+    suffix_pool_values,
+):
+    kv_count = lax.axis_size("kv")
+    seqs, width = queries.shape
+    heads = width // HEAD_SIZE
+    half_width = width // 2
+    reach, local_width = prompt_keys.shape
+    kv_heads = local_width // HEAD_SIZE
+    slots = page_table.shape[1]
+    page = suffix_pool_keys.shape[1]
+    half = seqs // 2
+    padded = half_width + LANES
+    prompts = prompt_of.reshape(-1)
+    smem = pl.BlockSpec(memory_space=pltpu.SMEM)
+    vmem = pl.BlockSpec(memory_space=pltpu.VMEM)
+    hbm = pl.BlockSpec(memory_space=pl.ANY)
+    core_swap = [(i, i ^ 1) for i in range(kv_count)]
+
+    def hop(value, mask):
+        return lax.ppermute(value, "kv", [(i, i ^ mask) for i in range(kv_count)])
+
+    def chip_hop(value, source, target):
+        return lax.ppermute(value, "kv", [(2 * source + c, 2 * target + c) for c in range(2)])
+
+    def struct(shape, dtype):
+        return jax.ShapeDtypeStruct(shape, dtype)
+
+    keys_other = lax.ppermute(prompt_keys, "kv", core_swap)
+    values_other = lax.ppermute(shared_prompt_values, "kv", core_swap)
+    rows_half = struct((seqs, half_width), jnp.bfloat16)
+    keep, send = pl.pallas_call(
+        pack_kernel, out_shape=(rows_half, rows_half), in_specs=[smem, vmem], name="pack"
+    )(prompts, queries)
+    received = hop(send, 1)
+    main, cross = pl.pallas_call(build_kernel, out_shape=(rows_half, rows_half), name="build")(
+        keep, received
+    )
+    main_far = hop(cross, 4)
+    main_near = hop(main, 2)
+    edge = kv_count // 4 - 1
+    others = [chip for chip in range(kv_count // 2) if chip != edge]
+    extra_queries = [cross] + [
+        chip_hop(cross if chip <= edge else main, chip, edge) for chip in others
+    ]
+    suffix_queries = queries.reshape(seqs, heads, HEAD_SIZE)
+
+    def suffix(first):
+        return pl.pallas_call(
+            functools.partial(suffix_kernel, first),
+            out_shape=(struct((half, width), jnp.float32), struct((half, width), jnp.float32)),
+            in_specs=[smem, smem, smem, vmem, hbm, hbm],
+            scratch_shapes=[
+                pltpu.SMEM((seqs,), jnp.int32),
+                pltpu.VMEM((half, slots, page, local_width), jnp.bfloat16),
+                pltpu.VMEM((half, slots, page, local_width), jnp.bfloat16),
+                pltpu.SemaphoreType.DMA((half,)),
+                pltpu.SemaphoreType.DMA((half,)),
+            ],
+            cost_estimate=pl.CostEstimate(
+                flops=4 * 1000 * half * heads * slots * page * HEAD_SIZE,
+                transcendentals=half * heads * slots * page,
+                bytes_accessed=4 * half * slots * page * local_width,
+            ),
+            name=f"suffix{first}",
+        )(prompts, page_table, suffix_len, suffix_queries, suffix_pool_keys, suffix_pool_values)
+
+    suffix_a = suffix(0)
+    main_both = hop(main_far, 2)
+    suffix_b = suffix(half)
+
+    steps = kv_heads // 2
+    columns = half_width // steps
+    row_block = pl.BlockSpec((seqs, columns), lambda j, core: (0, j))
+    cache_block = pl.BlockSpec((reach, HEAD_SIZE), lambda j, core: (0, core[0] * steps + j))
+    whole = pl.BlockSpec((seqs, padded), lambda j, core: (0, 0))
+    core = (lax.axis_index("kv") % 2).astype(jnp.int32).reshape(1)
+    coded = struct((seqs, padded), WIRE)
+    results = pl.pallas_call(
+        prompt_kernel,
+        grid_spec=pltpu.PrefetchScalarGridSpec(
+            num_scalar_prefetch=1,
+            grid=(steps,),
+            in_specs=[pl.BlockSpec(memory_space=pltpu.SMEM)] + [row_block] * 8 + [cache_block] * 4,
+            out_specs=[whole] * 8,
+            scratch_shapes=[
+                pltpu.VMEM((2 * reach, HEAD_SIZE), jnp.bfloat16),
+                pltpu.VMEM((2 * reach, HEAD_SIZE), jnp.bfloat16),
+                pltpu.VMEM((4 * seqs * columns // HEAD_SIZE, HEAD_SIZE), jnp.bfloat16),
+                pltpu.VMEM((seqs, LANES), jnp.float32),
+                pltpu.VMEM((3 * seqs, LANES), jnp.float32),
+                pltpu.VMEM((4 * seqs, LANES), jnp.float32),
+            ],
+        ),
+        out_shape=[struct((seqs, padded), jnp.float32)] + [coded] * 7,
+        name="prompt",
+    )(
+        core,
+        prompt_len,
+        main,
+        main_near,
+        main_far,
+        main_both,
+        *extra_queries,
+        prompt_keys,
+        keys_other,
+        shared_prompt_values,
+        values_other,
+    )
+    own, to_near, to_far, to_both = results[:4]
+    extra_local, extra_out = results[4], results[5:]
+    near, far, both = hop(to_near, 2), hop(to_far, 4), hop(to_both, 6)
+    extra_in = [chip_hop(value, edge, chip) for value, chip in zip(extra_out, others)]
+    joined_rows = struct((seqs, padded), jnp.float32)
+    kept, sent = pl.pallas_call(
+        merge_kernel,
+        out_shape=(joined_rows, joined_rows),
+        scratch_shapes=[pltpu.VMEM((seqs, padded), WIRE)],
+        name="merge",
+    )(own, near, far, both, extra_local, *extra_in)
+    returned = hop(sent, 1)
+    return pl.pallas_call(
+        final_kernel,
+        out_shape=struct((seqs, width), jnp.float32),
+        in_specs=[smem] + [vmem] * 6,
+        scratch_shapes=[pltpu.VMEM((seqs, width), jnp.float32)],
+        name="final",
+    )(prompts, kept, returned, *suffix_a, *suffix_b)
+
+
+def splits_heads(mesh, prompt_len):
+    prompts = prompt_len.shape[0] // mesh.shape["grp"]
+    return mesh.shape["sub"] == 1 and mesh.shape["kv"] == 4 * prompts and prompts == 2
+
+
 def solution(mesh):
     placed = (
         P(("grp", "kv"), "hd"),
@@ -202,6 +655,11 @@
         P(("grp", "kv", "sub"), None, "hd"),
         P(("grp", "kv", "sub"), None, "hd"),
     )
-    return jax.shard_map(
-        shards, mesh=mesh, in_specs=placed, out_specs=P(("grp", "kv"), "hd"), check_vma=False
-    )
+
+    def run(*arrays):
+        body = split_heads_shards if splits_heads(mesh, arrays[2]) else shards
+        return jax.shard_map(
+            body, mesh=mesh, in_specs=placed, out_specs=P(("grp", "kv"), "hd"), check_vma=False
+        )(*arrays)
+
+    return run

time: 139 us -> 70.4 us (0.51)
  matrix products: 48.7 us -> 0 us
  Pallas kernels: 0 us -> 30.7 us
  waiting for transfers between devices: 36.7 us -> 7.54 us
  local copies, waits for them, and re-layouts: 27.3 us -> 6.2 us
  starting transfers between devices: 13.3 us -> 25.3 us
  other arithmetic: 11.3 us -> 0 us
    dot_general x18 -> x0, matrix products: 48.7 us -> none  [the longest x8 22.2 us: attend_block(): lax.dot_general(head_query, head_keys, (((1,), (1,)), ((), ())), preferre...]
    all_to_all x3 -> x0, waiting for transfers between devices: 36.7 us -> none  [the longest x1 28.8 us: shards(): lax.all_to_all(prompt_out.reshape(kv_count, back_rows, row_width), 'kv',...]
    pallas_call x0 -> x7, Pallas kernels: none -> 30.7 us  [the longest x2 13.7 us: suffix(): pl.pallas_call(functools.partial(suffix_kernel, first), out_shape=(struct...]
    ppermute x0 -> x16, starting transfers between devices: none -> 25.3 us  [the longest x8 17.2 us: hop(): return lax.ppermute(value, 'kv', [(i, i ^ mask) for i in range(kv_count)])]
    gather x2 -> x0, local copies, waits for them, and re-layouts: 19.9 us -> none  [the longest x1 9.96 us: shards(): suffix_pool_values[page_table].reshape(seq_local, suffix_span, -1)]
    all_to_all x3 -> x0, starting transfers between devices: 13.3 us -> none  [the longest x1 6.37 us: shards(): lax.all_to_all(outgoing.reshape(kv_count, 2 * most_rows, row_width), 'kv'...]
    ppermute x0 -> x16, waiting for transfers between devices: none -> 7.54 us  [the longest x8 5.36 us: hop(): return lax.ppermute(value, 'kv', [(i, i ^ mask) for i in range(kv_count)])]
    reduce_sum x5 -> x0, other arithmetic: 5.94 us -> none  [the longest x2 5.36 us: attend_block(): totals = jnp.maximum(jnp.sum(weights, axis=2), 1.0)]
  transfers between devices with their start and end apart: 3 -> 16, of which waited for: 3 -> 5; matrix products, arithmetic and copies ran while one was open for 32% -> 4% of each run, Pallas kernels for 0% -> 24%
where the time goes in v1:
time: 70.4 us; the launch traced here: 70 us
  Pallas kernels  30.7 us (44%)
  starting transfers between devices  25.3 us (36%)
  waiting for transfers between devices  7.54 us (11%)
  local copies, waits for them, and re-layouts  6.2 us (9%)
    ppermute x8, starting transfers between devices, hop(): return lax.ppermute(value, 'kv', [(i, i ^ mask) for i in range(kv_count)])  17.2 us
    pallas_call x2, Pallas kernels, suffix(): pl.pallas_call(functools.partial(suffix_kernel, first), out_shape=(struct...  13.7 us
    pallas_call x1, Pallas kernels, split_heads_shards(): pl.pallas_call(prompt_kernel, grid_spec=pltpu.PrefetchScalarGridSpec(num_...  9.12 us
    ppermute x6, starting transfers between devices, chip_hop(): lax.ppermute(value, 'kv', [(2 * source + c, 2 * target + c) for c in rang...  7.59 us
    unnamed x34, local copies, waits for them, and re-layouts  6.2 us
    ppermute x8, waiting for transfers between devices, hop(): return lax.ppermute(value, 'kv', [(i, i ^ mask) for i in range(kv_count)])  5.36 us
    pallas_call x1, Pallas kernels, split_heads_shards(): pl.pallas_call(merge_kernel, out_shape=(joined_rows, joined_rows), scratc...  2.38 us
    pallas_call x1, Pallas kernels, split_heads_shards(): pl.pallas_call(final_kernel, out_shape=struct((seqs, width), jnp.float32)...  2.22 us
  transfers between devices with their start and end apart: 16, of which 5 were waited for; matrix products, arithmetic and copies ran while one was open for 4% of the time, Pallas kernels for 24%

profile of v1, /device:TPU:0, one launch (start us, length us, event | category | flops | bytes accessed | tf_op | source)
XLA Modules:
  0.0 70.0 jit_solution(17507748308708209201)
XLA Ops:
  0.0 0.5 collective-permute-start.7
  0.5 0.0 collective-permute-start.8
  0.5 1.8 %pack.1 = (bf16[16,2048]{1,0:T(8,128)(2,1)}, bf16[16,2048]{1,0:T(8,128)(2,1)}) custom-call(s32[128]{0:T(128)} %bitcast.7, bf16[16,4096]{1,0:T(8,128)(2,1)} %q_ref.1), custom_call_target="tpu_custom_call" | custom-call | tf_op jit(solution)/shard_map/pack/pallas_call | solution.py:542
  2.3 0.5 collective-permute-start
  2.8 1.8 %collective-permute-done.recv_ref = bf16[16,2048]{1,0:T(8,128)(2,1)S(1)} collective-permute-done((bf16[16,2048]{1,0:T(8,128)(2,1)}, bf16[16,2048]{1,0:T(8,128)(2,1)S(1)}, u32[]{:S(2)}, u32[]{:S(2)}) %collective-permute-start) | collective-permute-done | bytes 65568 | tf_op jit(solution)/shard_map/ppermute | solution.py:531
  4.6 0.6 copy-done.15
  5.2 1.5 %build.1 = (bf16[16,2048]{1,0:T(8,128)(2,1)}, bf16[16,2048]{1,0:T(8,128)(2,1)}) custom-call(bf16[16,2048]{1,0:T(8,128)(2,1)} %get-tuple-element.23.keep_ref, bf16[16,2048]{1,0:T(8,128)(2,1)} %copy-done.15), custom_call_target="tpu_custom_call" | custom-call | tf_op jit(solution)/shard_map/build/pallas_call | solution.py:546
  6.7 3.9 %collective-permute-start.2 = (bf16[16,2048]{1,0:T(8,128)(2,1)}, bf16[16,2048]{1,0:T(8,128)(2,1)S(1)}, u32[]{:S(2)}, u32[]{:S(2)}) collective-permute-start(bf16[16,2048]{1,0:T(8,128)(2,1)} %get-tuple-element.26.refs_4_), channel_id=1, source_target_pairs={{0,8},{2,10},{4,12},{6,14},{8,0},{10,2},{12,4},{14,6},{1,9},{3,11}... | collective-permute-start | bytes 196616 | tf_op jit(solution)/shard_map/ppermute | solution.py:531
  10.7 1.6 %collective-permute-start.1 = (bf16[16,2048]{1,0:T(8,128)(2,1)}, bf16[16,2048]{1,0:T(8,128)(2,1)S(1)}, u32[]{:S(2)}, u32[]{:S(2)}) collective-permute-start(bf16[16,2048]{1,0:T(8,128)(2,1)} %get-tuple-element.25.refs_0_), channel_id=1, source_target_pairs={{0,4},{2,6},{4,0},{6,2},{8,12},{10,14},{12,8},{14,10},{1,5},{3,7},... | collective-permute-start | bytes 196616 | tf_op jit(solution)/shard_map/ppermute | solution.py:531
  12.2 0.7 collective-permute-start.5
  12.9 1.3 %collective-permute-done.2.refs_2_ = bf16[16,2048]{1,0:T(8,128)(2,1)S(1)} collective-permute-done((bf16[16,2048]{1,0:T(8,128)(2,1)}, bf16[16,2048]{1,0:T(8,128)(2,1)S(1)}, u32[]{:S(2)}, u32[]{:S(2)}) %collective-permute-start.2) | collective-permute-done | bytes 65568 | tf_op jit(solution)/shard_map/ppermute | solution.py:531
  14.2 0.7 collective-permute-start.6
  14.8 0.3 collective-permute-done.1.refs_1_
  15.1 3.7 %collective-permute-start.4 = (bf16[16,2048]{1,0:T(8,128)(2,1)}, bf16[16,2048]{1,0:T(8,128)(2,1)S(1)}, u32[]{:S(2)}, u32[]{:S(2)}) collective-permute-start(bf16[16,2048]{1,0:T(8,128)(2,1)} %get-tuple-element.26.refs_4_), channel_id=1, source_target_pairs={{0,4},{2,6},{1,5},{3,7},{16,20},{18,22},{17,21},{19,23}} | collective-permute-start | bytes 196616 | tf_op jit(solution)/shard_map/ppermute | solution.py:534
  18.8 0.0 collective-permute-done.5.refs_6_
  18.8 0.2 collective-permute-start.3
  19.1 0.0 collective-permute-done.6.refs_7_
  19.1 2.2 %collective-permute-done.4.refs_5_ = bf16[16,2048]{1,0:T(8,128)(2,1)S(1)} collective-permute-done((bf16[16,2048]{1,0:T(8,128)(2,1)}, bf16[16,2048]{1,0:T(8,128)(2,1)S(1)}, u32[]{:S(2)}, u32[]{:S(2)}) %collective-permute-start.4) | collective-permute-done | bytes 65568 | tf_op jit(solution)/shard_map/ppermute | solution.py:534
  21.2 1.9 %collective-permute-done.3.refs_3_ = bf16[16,2048]{1,0:T(8,128)(2,1)S(1)} collective-permute-done((bf16[16,2048]{1,0:T(8,128)(2,1)S(1)}, bf16[16,2048]{1,0:T(8,128)(2,1)S(1)}, u32[]{:S(2)}, u32[]{:S(2)}) %collective-permute-start.3) | collective-permute-done | bytes 65568 | tf_op jit(solution)/shard_map/ppermute | solution.py:531
  23.2 0.0 collective-permute-done.7.refs_9_
  23.3 0.6 copy-done.14
  23.8 0.4 copy-done
  24.2 0.4 copy-done.1
  24.6 9.1 %prompt.1 = (f32[16,2176]{1,0:T(8,128)}, s16[16,2176]{1,0:T(8,128)(2,1)}, s16[16,2176]{1,0:T(8,128)(2,1)}, s16[16,2176]{1,0:T(8,128)(2,1)}, s16[16,2176]{1,0:T(8...) custom-call(s32[1]{0:T(128)} %bitcast.1.core_ref, s32[2]{0:T(128)} %length_ref.3, ...), custom_call_target="tpu_custom_call" | custom-call | tf_op jit(solution)/shard_map/prompt/pallas_call | solution.py:589
  33.7 0.8 %collective-permute-start.10 = (s16[16,2176]{1,0:T(8,128)(2,1)}, s16[16,2176]{1,0:T(8,128)(2,1)S(1)}, u32[]{:S(2)}, u32[]{:S(2)}) collective-permute-start(s16[16,2176]{1,0:T(8,128)(2,1)} %get-tuple-element.29), channel_id=1, source_target_pairs={{0,8},{2,10},{4,12},{6,14},{8,0},{10,2},{12,4},{14,6},{1,9},{3,11}... | collective-permute-start | bytes 208904 | tf_op jit(solution)/shard_map/ppermute | solution.py:531
  34.5 1.6 %copy.12 = bf16[2,8,32,128]{3,2,1,0:T(8,128)(2,1)} copy(bf16[2,8,32,128]{3,1,2,0:T(8,128)(2,1)} %bitcast.4) | data formatting | bytes 262144
  36.0 1.4 %copy.10.table_ref = s32[16,8]{1,0:T(8,128)} copy(s32[16,8]{0,1:T(8,128)} %param.13) | data formatting | bytes 1024 | tf_op args[4]
  37.4 6.2 %collective-permute-start.11 = (s16[16,2176]{1,0:T(8,128)(2,1)}, s16[16,2176]{1,0:T(8,128)(2,1)S(1)}, u32[]{:S(2)}, u32[]{:S(2)}) collective-permute-start(s16[16,2176]{1,0:T(8,128)(2,1)} %get-tuple-element.30), channel_id=1, source_target_pairs={{0,12},{2,14},{4,8},{6,10},{8,4},{10,6},{12,0},{14,2},{1,13},{3,15... | collective-permute-start | bytes 208904 | tf_op jit(solution)/shard_map/ppermute | solution.py:531
  43.6 1.3 %collective-permute-start.12 = (s16[16,2176]{1,0:T(8,128)(2,1)}, s16[16,2176]{1,0:T(8,128)(2,1)S(1)}, u32[]{:S(2)}, u32[]{:S(2)}) collective-permute-start(s16[16,2176]{1,0:T(8,128)(2,1)} %get-tuple-element.32), channel_id=1, source_target_pairs={{4,0},{6,2},{5,1},{7,3},{20,16},{22,18},{21,17},{23,19}} | collective-permute-start | bytes 208904 | tf_op jit(solution)/shard_map/ppermute | solution.py:534
  44.9 0.7 collective-permute-start.13
  45.6 0.7 collective-permute-start.14
  46.2 0.0 collective-permute-done.10.far_ref
  46.2 4.0 %collective-permute-start.9 = (s16[16,2176]{1,0:T(8,128)(2,1)}, s16[16,2176]{1,0:T(8,128)(2,1)S(1)}, u32[]{:S(2)}, u32[]{:S(2)}) collective-permute-start(s16[16,2176]{1,0:T(8,128)(2,1)} %get-tuple-element.28), channel_id=1, source_target_pairs={{0,4},{2,6},{4,0},{6,2},{8,12},{10,14},{12,8},{14,10},{1,5},{3,7},... | collective-permute-start | bytes 208904 | tf_op jit(solution)/shard_map/ppermute | solution.py:531
  50.2 6.9 %suffix0.1 = (f32[8,4096]{1,0:T(8,128)}, f32[8,4096]{1,0:T(8,128)}) custom-call(s32[128]{0:T(128)} %bitcast.8, s32[16,8]{1,0:T(8,128)} %copy.10.table_ref, s32[16]{0:T(128)} %length_ref.5, bf16[16,32,128]{2,1,0:T(8,128)(2,1)} %bitcast.5, bf16[128,64,512]{2,1,0:T(8,128)(2,1)} %k_hbm.3, bf16[128,64,512]{2,1,0:T(8,128)(2,1)} %v_hbm.3), custom_call_target="tpu_custom_call" | custom-call | flops 67108864000 | bytes 8388608 | tf_op jit(solution)/shard_map/suffix0/pallas_call | solution.py:559
  57.1 0.0 collective-permute-done.12.x_a
  57.1 0.0 collective-permute-done.13.x_b
  57.2 0.0 collective-permute-done.9.near_ref
  57.2 0.5 copy-done.4
  57.7 0.0 copy-done.5
  57.8 0.0 copy-done.6
  57.8 0.0 copy-done.7
  57.8 0.0 copy-done.8
  57.9 2.4 %merge.1 = (f32[16,2176]{1,0:T(8,128)}, f32[16,2176]{1,0:T(8,128)}) custom-call(f32[16,2176]{1,0:T(8,128)} %get-tuple-element.27.own_ref, s16[16,2176]{1,0:T(8,128)(2,1)} %copy-done.8, s16[16,2176]{1,0:T(8,128)(2,1)} %copy-done.3, s16[16,2176]{1,0:T(8,128)(2,1)} %copy-done.4, s16[16,2176]{1,0:T(8,128)(2,1)} %get-tuple-element.31.x_local, ...), custom_call_target="tpu_custom_call" | custom-call | tf_op jit(solution)/shard_map/merge/pallas_call | solution.py:625
  60.2 0.0 collective-permute-start.15
  60.2 6.9 %suffix8.1 = (f32[8,4096]{1,0:T(8,128)}, f32[8,4096]{1,0:T(8,128)}) custom-call(s32[128]{0:T(128)} %bitcast.9, s32[16,8]{1,0:T(8,128)} %copy.10.table_ref, s32[16]{0:T(128)} %length_ref.5, bf16[16,32,128]{2,1,0:T(8,128)(2,1)} %bitcast.6, bf16[128,64,512]{2,1,0:T(8,128)(2,1)} %k_hbm.3, bf16[128,64,512]{2,1,0:T(8,128)(2,1)} %v_hbm.3), custom_call_target="tpu_custom_call" | custom-call | flops 67108864000 | bytes 8388608 | tf_op jit(solution)/shard_map/suffix8/pallas_call | solution.py:559
  67.1 0.0 collective-permute-done.15.recv_ref
  67.1 0.6 copy-done.2
  67.8 2.2 %final.1 = f32[16,4096]{1,0:T(8,128)} custom-call(s32[128]{0:T(128)} %bitcast.10, f32[16,2176]{1,0:T(8,128)} %get-tuple-element.35.keep_ref, f32[16,2176]{1,0:T(8,128)} %copy-done.2, f32[8,4096]{1,0:T(8,128)} %get-tuple-element.37.so_a, f32[8,4096]{1,0:T(8,128)} %get-tuple-element.38.sl_a, f32[8,4096]{1,0:T(8,128)} %get-tuple-element.39.so_b, ...), custom_call_target="tpu_custom_call" | custom-call | tf_op jit(solution)/shard_map/final/pallas_call | solution.py:632
  (25 shorter events, 0.1 us)
Async XLA Ops:
  0.0 23.2 %collective-permute-start.7 = (bf16[1024,512]{1,0:T(8,128)(2,1)}, bf16[1024,512]{1,0:T(8,128)(2,1)S(1)}, u32[]{:S(2)}, u32[]{:S(2)}) collective-permute-start(bf16[1024,512]{1,0:T(8,128)(2,1)} %refs_8_.1), channel_id=1, source_target_pairs={{0,2},{2,0},{4,6},{6,4},{8,10},{10,8},{12,14},{14,12},{1,3},{3,1},... | collective-permute-start | bytes 3145736 | tf_op jit(solution)/shard_map/ppermute | solution.py:539
  0.5 22.7 %collective-permute-start.8 = (bf16[1024,512]{1,0:T(8,128)(2,1)}, bf16[1024,512]{1,0:T(8,128)(2,1)S(1)}, u32[]{:S(2)}, u32[]{:S(2)}) collective-permute-start(bf16[1024,512]{1,0:T(8,128)(2,1)} %refs_10_.1), channel_id=1, source_target_pairs={{0,2},{2,0},{4,6},{6,4},{8,10},{10,8},{12,14},{14,12},{1,3},{3,1},... | collective-permute-start | bytes 3145736 | tf_op jit(solution)/shard_map/ppermute | solution.py:540
  2.3 2.3 %collective-permute-start = (bf16[16,2048]{1,0:T(8,128)(2,1)}, bf16[16,2048]{1,0:T(8,128)(2,1)S(1)}, u32[]{:S(2)}, u32[]{:S(2)}) collective-permute-start(bf16[16,2048]{1,0:T(8,128)(2,1)} %get-tuple-element.24), channel_id=1, source_target_pairs={{0,2},{2,0},{4,6},{6,4},{8,10},{10,8},{12,14},{14,12},{1,3},{3,1},... | collective-permute-start | bytes 196616 | tf_op jit(solution)/shard_map/ppermute | solution.py:531
  4.6 0.6 copy-start.15
  6.7 7.5 %collective-permute-start.2 = (bf16[16,2048]{1,0:T(8,128)(2,1)}, bf16[16,2048]{1,0:T(8,128)(2,1)S(1)}, u32[]{:S(2)}, u32[]{:S(2)}) collective-permute-start(bf16[16,2048]{1,0:T(8,128)(2,1)} %get-tuple-element.26.refs_4_), channel_id=1, source_target_pairs={{0,8},{2,10},{4,12},{6,14},{8,0},{10,2},{12,4},{14,6},{1,9},{3,11}... | collective-permute-start | bytes 196616 | tf_op jit(solution)/shard_map/ppermute | solution.py:531
  10.7 4.5 %collective-permute-start.1 = (bf16[16,2048]{1,0:T(8,128)(2,1)}, bf16[16,2048]{1,0:T(8,128)(2,1)S(1)}, u32[]{:S(2)}, u32[]{:S(2)}) collective-permute-start(bf16[16,2048]{1,0:T(8,128)(2,1)} %get-tuple-element.25.refs_0_), channel_id=1, source_target_pairs={{0,4},{2,6},{4,0},{6,2},{8,12},{10,14},{12,8},{14,10},{1,5},{3,7},... | collective-permute-start | bytes 196616 | tf_op jit(solution)/shard_map/ppermute | solution.py:531
  12.2 6.6 %collective-permute-start.5 = (bf16[16,2048]{1,0:T(8,128)(2,1)}, bf16[16,2048]{1,0:T(8,128)(2,1)S(1)}, u32[]{:S(2)}, u32[]{:S(2)}) collective-permute-start(bf16[16,2048]{1,0:T(8,128)(2,1)} %get-tuple-element.25.refs_0_), channel_id=1, source_target_pairs={{8,4},{10,6},{9,5},{11,7},{24,20},{26,22},{25,21},{27,23}} | collective-permute-start | bytes 196616 | tf_op jit(solution)/shard_map/ppermute | solution.py:534
  14.2 9.0 %copy-start.9 = (bf16[16,2048]{1,0:T(8,128)(2,1)}, bf16[16,2048]{1,0:T(8,128)(2,1)S(1)}, u32[]{:S(2)}) copy-start(bf16[16,2048]{1,0:T(8,128)(2,1)S(1)} %collective-permute-done.2.refs_2_) | copy-start | bytes 196612
  14.2 4.9 %collective-permute-start.6 = (bf16[16,2048]{1,0:T(8,128)(2,1)}, bf16[16,2048]{1,0:T(8,128)(2,1)S(1)}, u32[]{:S(2)}, u32[]{:S(2)}) collective-permute-start(bf16[16,2048]{1,0:T(8,128)(2,1)} %get-tuple-element.25.refs_0_), channel_id=1, source_target_pairs={{12,4},{14,6},{13,5},{15,7},{28,20},{30,22},{29,21},{31,23}} | collective-permute-start | bytes 196616 | tf_op jit(solution)/shard_map/ppermute | solution.py:534
  15.1 8.1 %copy-start.10 = (bf16[16,2048]{1,0:T(8,128)(2,1)}, bf16[16,2048]{1,0:T(8,128)(2,1)S(1)}, u32[]{:S(2)}) copy-start(bf16[16,2048]{1,0:T(8,128)(2,1)S(1)} %collective-permute-done.1.refs_1_) | copy-start | bytes 196612
  15.1 6.1 %collective-permute-start.4 = (bf16[16,2048]{1,0:T(8,128)(2,1)}, bf16[16,2048]{1,0:T(8,128)(2,1)S(1)}, u32[]{:S(2)}, u32[]{:S(2)}) collective-permute-start(bf16[16,2048]{1,0:T(8,128)(2,1)} %get-tuple-element.26.refs_4_), channel_id=1, source_target_pairs={{0,4},{2,6},{1,5},{3,7},{16,20},{18,22},{17,21},{19,23}} | collective-permute-start | bytes 196616 | tf_op jit(solution)/shard_map/ppermute | solution.py:534
  18.8 4.4 %copy-start.11 = (bf16[16,2048]{1,0:T(8,128)(2,1)}, bf16[16,2048]{1,0:T(8,128)(2,1)S(1)}, u32[]{:S(2)}) copy-start(bf16[16,2048]{1,0:T(8,128)(2,1)S(1)} %collective-permute-done.5.refs_6_) | copy-start | bytes 196612
  18.8 4.3 %collective-permute-start.3 = (bf16[16,2048]{1,0:T(8,128)(2,1)S(1)}, bf16[16,2048]{1,0:T(8,128)(2,1)S(1)}, u32[]{:S(2)}, u32[]{:S(2)}) collective-permute-start(bf16[16,2048]{1,0:T(8,128)(2,1)S(1)} %collective-permute-done.2.refs_2_), channel_id=1, source_target_pairs={{0,4},{2,6},{4,0},{6,2},{8,12},{10,14},{12,8},{14,10},{1,5},{3,7},... | collective-permute-start | bytes 196616 | tf_op jit(solution)/shard_map/ppermute | solution.py:531
  19.1 4.2 %copy-start.12 = (bf16[16,2048]{1,0:T(8,128)(2,1)}, bf16[16,2048]{1,0:T(8,128)(2,1)S(1)}, u32[]{:S(2)}) copy-start(bf16[16,2048]{1,0:T(8,128)(2,1)S(1)} %collective-permute-done.6.refs_7_) | copy-start | bytes 196612
  21.2 2.0 %copy-start.13 = (bf16[16,2048]{1,0:T(8,128)(2,1)}, bf16[16,2048]{1,0:T(8,128)(2,1)S(1)}, u32[]{:S(2)}) copy-start(bf16[16,2048]{1,0:T(8,128)(2,1)S(1)} %collective-permute-done.4.refs_5_) | copy-start | bytes 196612
  23.2 0.6 copy-start.14
  23.2 1.0 %copy-start = (bf16[1024,512]{1,0:T(8,128)(2,1)}, bf16[1024,512]{1,0:T(8,128)(2,1)S(1)}, u32[]{:S(2)}) copy-start(bf16[1024,512]{1,0:T(8,128)(2,1)S(1)} %collective-permute-done.7.refs_9_) | copy-start | bytes 3145732
  23.2 1.4 %copy-start.1 = (bf16[1024,512]{1,0:T(8,128)(2,1)}, bf16[1024,512]{1,0:T(8,128)(2,1)S(1)}, u32[]{:S(2)}) copy-start(bf16[1024,512]{1,0:T(8,128)(2,1)S(1)} %collective-permute-done.8.refs_11_) | copy-start | bytes 3145732
  33.7 12.6 %collective-permute-start.10 = (s16[16,2176]{1,0:T(8,128)(2,1)}, s16[16,2176]{1,0:T(8,128)(2,1)S(1)}, u32[]{:S(2)}, u32[]{:S(2)}) collective-permute-start(s16[16,2176]{1,0:T(8,128)(2,1)} %get-tuple-element.29), channel_id=1, source_target_pairs={{0,8},{2,10},{4,12},{6,14},{8,0},{10,2},{12,4},{14,6},{1,9},{3,11}... | collective-permute-start | bytes 208904 | tf_op jit(solution)/shard_map/ppermute | solution.py:531
  37.4 19.7 %collective-permute-start.11 = (s16[16,2176]{1,0:T(8,128)(2,1)}, s16[16,2176]{1,0:T(8,128)(2,1)S(1)}, u32[]{:S(2)}, u32[]{:S(2)}) collective-permute-start(s16[16,2176]{1,0:T(8,128)(2,1)} %get-tuple-element.30), channel_id=1, source_target_pairs={{0,12},{2,14},{4,8},{6,10},{8,4},{10,6},{12,0},{14,2},{1,13},{3,15... | collective-permute-start | bytes 208904 | tf_op jit(solution)/shard_map/ppermute | solution.py:531
  43.6 13.5 %collective-permute-start.12 = (s16[16,2176]{1,0:T(8,128)(2,1)}, s16[16,2176]{1,0:T(8,128)(2,1)S(1)}, u32[]{:S(2)}, u32[]{:S(2)}) collective-permute-start(s16[16,2176]{1,0:T(8,128)(2,1)} %get-tuple-element.32), channel_id=1, source_target_pairs={{4,0},{6,2},{5,1},{7,3},{20,16},{22,18},{21,17},{23,19}} | collective-permute-start | bytes 208904 | tf_op jit(solution)/shard_map/ppermute | solution.py:534
  44.9 12.3 %collective-permute-start.13 = (s16[16,2176]{1,0:T(8,128)(2,1)}, s16[16,2176]{1,0:T(8,128)(2,1)S(1)}, u32[]{:S(2)}, u32[]{:S(2)}) collective-permute-start(s16[16,2176]{1,0:T(8,128)(2,1)} %get-tuple-element.33), channel_id=1, source_target_pairs={{4,8},{6,10},{5,9},{7,11},{20,24},{22,26},{21,25},{23,27}} | collective-permute-start | bytes 208904 | tf_op jit(solution)/shard_map/ppermute | solution.py:534
  45.6 11.6 %collective-permute-start.14 = (s16[16,2176]{1,0:T(8,128)(2,1)}, s16[16,2176]{1,0:T(8,128)(2,1)S(1)}, u32[]{:S(2)}, u32[]{:S(2)}) collective-permute-start(s16[16,2176]{1,0:T(8,128)(2,1)} %get-tuple-element.34), channel_id=1, source_target_pairs={{4,12},{6,14},{5,13},{7,15},{20,28},{22,30},{21,29},{23,31}} | collective-permute-start | bytes 208904 | tf_op jit(solution)/shard_map/ppermute | solution.py:534
  46.2 10.9 %copy-start.3 = (s16[16,2176]{1,0:T(8,128)(2,1)}, s16[16,2176]{1,0:T(8,128)(2,1)S(1)}, u32[]{:S(2)}) copy-start(s16[16,2176]{1,0:T(8,128)(2,1)S(1)} %collective-permute-done.10.far_ref) | copy-start | bytes 208900
  46.2 10.9 %collective-permute-start.9 = (s16[16,2176]{1,0:T(8,128)(2,1)}, s16[16,2176]{1,0:T(8,128)(2,1)S(1)}, u32[]{:S(2)}, u32[]{:S(2)}) collective-permute-start(s16[16,2176]{1,0:T(8,128)(2,1)} %get-tuple-element.28), channel_id=1, source_target_pairs={{0,4},{2,6},{4,0},{6,2},{8,12},{10,14},{12,8},{14,10},{1,5},{3,7},... | collective-permute-start | bytes 208904 | tf_op jit(solution)/shard_map/ppermute | solution.py:531
  57.1 0.6 copy-start.4
  57.1 0.6 copy-start.5
  57.2 0.6 copy-start.6
  57.2 0.7 copy-start.7
  57.2 0.7 copy-start.8
  60.2 6.9 %collective-permute-start.15 = (f32[16,2176]{1,0:T(8,128)}, f32[16,2176]{1,0:T(8,128)S(1)}, u32[]{:S(2)}, u32[]{:S(2)}) collective-permute-start(f32[16,2176]{1,0:T(8,128)} %get-tuple-element.36), channel_id=1, source_target_pairs={{0,2},{2,0},{4,6},{6,4},{8,10},{10,8},{12,14},{14,12},{1,3},{3,1},... | collective-permute-start | bytes 417800 | tf_op jit(solution)/shard_map/ppermute | solution.py:531
  67.1 0.7 copy-start.2
